TPU v7x, 128 devices: a whole 4x4x4 slice. The times are simulated.
128 devices in a mesh: sp: 8 (over x, y_lo), ep: 16 (over z, y_hi, core).
Axes of the slice: x: 4, y: 4 (y_hi: 2, y_lo: 2; y = y_hi * 2 + y_lo), z: 4, core: 2. Of those that a mesh axis runs over, the one named last changes fastest.
Arguments:
- residual: bfloat16 [16384, 4096], P(('sp', 'ep')), may hold values from -40 to 40
- queries: bfloat16 [16384, 4096], P(('sp', 'ep')), may hold values from -6 to 6
- key_rows: bfloat16 [16384, 1024], P(('sp', 'ep')), may hold values from -6 to 6
- value_rows: bfloat16 [16384, 1024], P(('sp', 'ep')), may hold values from -6 to 6
- visible: int32 [128, 9], replicated, may hold values from 0 to 1, as said below
- out_proj: bfloat16 [4096, 4096], P(('sp', 'ep')), may hold values from -0.09375 to 0.09375
- norm_gain: float32 [4096], replicated, may hold values from 0.5 to 1.5
- expert_ids: int32 [16384, 2], P(('sp', 'ep')), may hold values from 0 to 7, all different within a row; in each aligned block of 128 rows (0 to 127, 128 to 255, ...) at most 40 rows name the same one
- route_weight: float32 [16384, 2], P(('sp', 'ep')), may hold values from 0.2 to 1
- expert_gate: bfloat16 [2, 7168, 4096], P(None, 'ep'), may hold values from -0.09375 to 0.09375
- expert_up: bfloat16 [2, 7168, 4096], P(None, 'ep'), may hold values from -0.09375 to 0.09375
- expert_down: bfloat16 [2, 7168, 4096], P(None, 'ep'), may hold values from -0.0625 to 0.0625
Outputs:
- layer_out: bfloat16 [16384, 4096], P(('sp', 'ep'))
Inputs may be any that keep to these rules, and one draw needn't show every extreme that they name: The sequence is packed with documents that are runs of whole blocks of 128 tokens, the first of them 9 blocks or longer; visible[q, d] is 1 exactly when block q - d exists and lies in the document of block q, so visible[q, 0] = 1. `expert_ids`: each token names two different experts. Among the 128 tokens of one block no expert is named by more than 40 tokens.
All inputs are finite; a program needn't handle non-finite values.
Results may differ from a plain program's by a relative error of at most 0.0065.
Values may be sent and summed in bfloat16 or wider, within the bound.
No kernel may reach another device: no remote copies, remote signals or barrier semaphores. Data moves between devices by JAX's collectives and lax.ppermute only.
A program may use at most 128 MiB of HBM per device.

v0:
```python
import math

import jax
import jax.numpy as jnp
from jax import lax
from jax.experimental import pallas as pl
from jax.experimental.pallas import tpu as pltpu
from jax.sharding import Mesh
from jax.sharding import PartitionSpec as P

HEAD = 128
CAP = 40
SIZES = (4, 2, 4, 2, 2)
AXES = ("x", "yl", "z", "h", "c")
EP = ("z", "h", "c")


def flat(coords):
    place = 0
    for size, coord in zip(SIZES, coords):
        place = place * size + coord
    return place


def sent(value, rule):
    pairs = []
    for source in range(math.prod(SIZES)):
        rest, coords = source, []
        for size in reversed(SIZES):
            coords.append(rest % size)
            rest //= size
        cx, cyl, cz, ch, cc = reversed(coords)
        x, y, z, core = rule(cx, 2 * ch + cyl, cz, cc)
        pairs.append((source, flat((x % 4, y % 2, z % 4, y % 4 // 2, core))))
    return lax.ppermute(value, AXES, pairs)


def moved(value, x=0, y=0, z=0):
    return sent(value, lambda cx, cy, cz, cc: (cx + x, cy + y, cz + z, cc))


def crossed(value):
    return sent(value, lambda cx, cy, cz, cc: (cx, cy, cz, 1 - cc))


def mate(place, pairing):
    return place + (1 if (place + pairing) % 2 == 0 else -1)


def to_mate(value, along_x, along_z, switch):
    def rule(cx, cy, cz, cc):
        goal = 1 - cc if switch else cc
        return (mate(cx, goal) if along_x else cx, cy, mate(cz, goal) if along_z else cz, goal)

    return sent(value, rule)


def from_mate(value, along_x, along_z, switch):
    def rule(cx, cy, cz, cc):
        goal = 1 - cc if switch else cc
        return (mate(cx, cc) if along_x else cx, cy, mate(cz, cc) if along_z else cz, goal)

    return sent(value, rule)


def later(value, blocks):
    count = math.prod(SIZES)
    return lax.ppermute(value, AXES, [(s, s + blocks) for s in range(count - blocks)])


def half_of(value, which):
    width = value.shape[-1] // 2
    return lax.dynamic_slice_in_dim(value, which * width, width, value.ndim - 1)


def by_core(first, own, other, axis):
    return jnp.where(
        first,
        jnp.concatenate([own, other], axis=axis),
        jnp.concatenate([other, own], axis=axis),
    )


def attend_kernel(seen_ref, query_ref, *refs):
    key_refs, value_refs, out_ref = refs[:5], refs[5:10], refs[10]
    keys = jnp.concatenate([ref[...] for ref in key_refs], axis=0)
    values = jnp.concatenate([ref[...] for ref in value_refs], axis=0)
    factor = math.log2(math.e) / math.sqrt(HEAD)
    tokens = 128
    row = lax.broadcasted_iota(jnp.int32, (tokens, tokens), 0)
    col = lax.broadcasted_iota(jnp.int32, (tokens, tokens), 1)
    causal = jnp.where(col <= row, 0.0, -1e30)
    for block in range(2):
        here = slice(block * tokens, (block + 1) * tokens)
        key_window = keys[block * tokens : (block + 9) * tokens]
        value_window = values[block * tokens : (block + 9) * tokens]
        hidden = [
            jnp.full((tokens, tokens), jnp.where(seen_ref[block, 8 - place] > 0, 0.0, -1e30))
            for place in range(8)
        ]
        bias = jnp.concatenate(hidden + [causal], axis=1)
        query = jnp.concatenate(
            [query_ref[here, head * HEAD : (head + 1) * HEAD] for head in range(4)], axis=0
        )
        scores = lax.dot_general(
            query, key_window, (((1,), (1,)), ((), ())), preferred_element_type=jnp.float32
        )
        weights, totals = [], []
        for head in range(4):
            score = scores[head * tokens : (head + 1) * tokens] + bias
            peak = jnp.max(score, axis=1, keepdims=True)
            weight = jnp.exp2((score - peak) * factor)
            totals.append(jnp.sum(weight, axis=1, keepdims=True))
            weights.append(weight.astype(jnp.bfloat16))
        mixed = jnp.dot(
            jnp.concatenate(weights, axis=0), value_window, preferred_element_type=jnp.float32
        )
        for head in range(4):
            result = mixed[head * tokens : (head + 1) * tokens] / totals[head]
            lanes = slice(head // 2 * HEAD, head // 2 * HEAD + HEAD)
            out_ref[0, head % 2, here, lanes] = result.astype(jnp.bfloat16)


def attend(seen, query, windows):
    key_specs = [pl.BlockSpec((256, HEAD), lambda j: (0, j)) for _ in windows]
    value_specs = [pl.BlockSpec((256, HEAD), lambda j: (0, 4 + j)) for _ in windows]
    return pl.pallas_call(
        attend_kernel,
        grid=(4,),
        in_specs=[
            pl.BlockSpec(memory_space=pltpu.SMEM),
            pl.BlockSpec((256, 4 * HEAD), lambda j: (0, j)),
            *key_specs,
            *value_specs,
        ],
        out_specs=pl.BlockSpec((1, 2, 256, 256), lambda j: (j // 2, 0, 0, j % 2)),
        out_shape=jax.ShapeDtypeStruct((2, 2, 256, 512), jnp.bfloat16),
        name="attend",
        cost_estimate=pl.CostEstimate(
            flops=6_000_000_000, transcendentals=5_000_000, bytes_accessed=6_000_000
        ),
    )(seen, query, *windows, *windows)


def in_order(pieces, own_index):
    count = len(pieces)
    table = jnp.zeros((count, *pieces[0].shape), pieces[0].dtype)
    for step, piece in enumerate(pieces):
        table = lax.dynamic_update_index_in_dim(table, piece, (own_index - step) % count, 0)
    return table


def project_kernel(core_ref, *refs):
    mine, mine_other, theirs, theirs_other, rows_own, rows_other, straight_ref, switch_ref = refs
    left = jnp.concatenate([mine[0], mine_other[0]], axis=0)
    right = jnp.concatenate([theirs[0], theirs_other[0]], axis=0)
    product = jnp.dot(left, rows_own[0], preferred_element_type=jnp.float32)
    product += jnp.dot(right, rows_other[0], preferred_element_type=jnp.float32)
    product = product.astype(jnp.bfloat16)
    straight_ref[...] = product[:128]
    switch_ref[...] = product[128:]


def project(core, own_heads, other_heads, rows):
    columns = 512
    own_heads = own_heads.reshape(2, 128, 512)
    other_heads = other_heads.reshape(2, 128, 512)
    here = pl.BlockSpec((1, 128, 512), lambda n, core: (core[0], 0, 0))
    there = pl.BlockSpec((1, 128, 512), lambda n, core: (1 - core[0], 0, 0))
    out = pl.BlockSpec((128, columns), lambda n, core: (0, n))
    shape = jax.ShapeDtypeStruct((128, rows.shape[2]), jnp.bfloat16)
    return pl.pallas_call(
        project_kernel,
        grid_spec=pltpu.PrefetchScalarGridSpec(
            num_scalar_prefetch=1,
            grid=(rows.shape[2] // columns,),
            in_specs=[
                here,
                there,
                here,
                there,
                pl.BlockSpec((1, 512, columns), lambda n, core: (core[0], 0, n)),
                pl.BlockSpec((1, 512, columns), lambda n, core: (1 - core[0], 0, n)),
            ],
            out_specs=[out, out],
        ),
        out_shape=[shape, shape],
        name="project",
        cost_estimate=pl.CostEstimate(
            flops=1_073_741_824, transcendentals=0, bytes_accessed=6_000_000
        ),
    )(core.reshape(1), own_heads, own_heads, other_heads, other_heads, rows, rows)


def expert_kernel(*refs):
    slot_refs, (gate_ref, up_ref, down_ref, own_ref, other_ref) = refs[:16], refs[16:21]
    gate_sum, up_sum, act = refs[21:]
    step = pl.program_id(0)
    contract = (((1,), (1,)), ((), ()))

    @pl.when(step < 4)
    def _():
        slots = jnp.concatenate([ref[...] for ref in slot_refs], axis=0)
        gate = lax.dot_general(slots, gate_ref[0], contract, preferred_element_type=jnp.float32)
        up = lax.dot_general(slots, up_ref[0], contract, preferred_element_type=jnp.float32)

        @pl.when(step == 0)
        def _():
            gate_sum[...] = gate
            up_sum[...] = up

        @pl.when(step > 0)
        def _():
            gate_sum[...] += gate
            up_sum[...] += up

        @pl.when(step == 3)
        def _():
            value = gate_sum[...]
            act[...] = (value / (1.0 + jnp.exp(-value)) * up_sum[...]).astype(jnp.bfloat16)

    @pl.when(step >= 4)
    def _():
        result = jnp.dot(act[...], down_ref[0], preferred_element_type=jnp.float32)
        result = result.astype(jnp.bfloat16)
        half = result.shape[0] // 2
        own_ref[...] = result[:half]
        other_ref[...] = result[half:]


def expert(which, pieces, gate, up, down):
    slots, width = pieces[0].shape
    hidden = gate.shape[1]
    chunk = width // 4
    count = len(pieces) * slots
    early = lambda step: jnp.minimum(step, 3)
    late = lambda step: jnp.maximum(step - 4, 0)
    out = pl.BlockSpec((count // 2, chunk), lambda step: (0, late(step)))
    shape = jax.ShapeDtypeStruct((count // 2, width), jnp.bfloat16)
    return pl.pallas_call(
        expert_kernel,
        grid=(8,),
        in_specs=[
            *[pl.BlockSpec((slots, chunk), lambda step: (0, early(step))) for _ in pieces],
            pl.BlockSpec((1, hidden, chunk), lambda step: (which, 0, early(step))),
            pl.BlockSpec((1, hidden, chunk), lambda step: (which, 0, early(step))),
            pl.BlockSpec((1, hidden, chunk), lambda step: (which, 0, late(step))),
        ],
        out_specs=[out, out],
        out_shape=[shape, shape],
        scratch_shapes=[
            pltpu.VMEM((count, hidden), jnp.float32),
            pltpu.VMEM((count, hidden), jnp.float32),
            pltpu.VMEM((count, hidden), jnp.bfloat16),
        ],
        name="expert",
        cost_estimate=pl.CostEstimate(
            flops=7_000_000_000, transcendentals=300_000, bytes_accessed=22_000_000
        ),
    )(*pieces, gate, up, down)


def total(*terms):
    return sum(term.astype(jnp.float32) for term in terms).astype(jnp.bfloat16)


def gather_slots(own):
    flip = moved(own, y=2)
    up1, up3, up2 = moved(own, z=1), moved(own, z=3), moved(own, z=2)
    flip1, flip3, flip2 = moved(flip, z=1), moved(flip, z=3), moved(up2, y=2)
    pieces = [own, up1, up2, up3, flip, flip1, flip2, flip3]
    return pieces + [crossed(piece) for piece in pieces]


def return_sums(own_part, other_part):
    swapped = crossed(other_part)

    def owed(place):
        rows = slice(place * CAP, (place + 1) * CAP)
        return total(own_part[rows], swapped[rows])

    side1, side3 = moved(owed(5), z=3), moved(owed(7), z=1)
    far = moved(owed(6), y=2)
    near1, near3 = moved(owed(1), z=3), moved(owed(3), z=1)
    across = moved(total(owed(4), side1, side3), y=2)
    twice = moved(total(owed(2), far), z=2)
    return sum(t.astype(jnp.float32) for t in (owed(0), near1, near3, across, twice))


def local(
    residual,
    queries,
    key_rows,
    value_rows,
    visible,
    out_proj,
    norm_gain,
    expert_ids,
    route_weight,
    expert_gate,
    expert_up,
    expert_down,
):
    core = lax.axis_index("c")
    first = core == 0
    tokens = residual.shape[0]
    place_x, place_z = lax.axis_index("x"), lax.axis_index("z")
    place_y = 2 * lax.axis_index("h") + lax.axis_index("yl")

    kv_own = jnp.concatenate([half_of(key_rows, core), half_of(value_rows, core)], axis=1)
    kv_give = jnp.concatenate([half_of(key_rows, 1 - core), half_of(value_rows, 1 - core)], axis=1)
    kv_two = by_core(first, kv_own, crossed(kv_give), 0)
    query_two = by_core(first, half_of(queries, core), crossed(half_of(queries, 1 - core)), 0)
    windows = [later(kv_two, blocks) for blocks in (8, 6, 4, 2)] + [kv_two]

    columns = out_proj.shape[1] // 2
    rows = by_core(first, half_of(out_proj, core), crossed(half_of(out_proj, 1 - core)), 0)
    rows = in_order([rows, moved(rows, z=2)], place_z // 2)
    rows = in_order([rows] + [moved(rows, y=step) for step in (1, 2, 3)], place_y)
    rows = rows.reshape(2, 2, 2, 2 * out_proj.shape[0], columns)
    rows = rows.transpose(1, 2, 0, 3, 4).reshape(-1, columns)
    rows = in_order([rows, moved(rows, x=2)], place_x // 2)

    chip_block = lax.axis_index(AXES) - core
    seen = lax.dynamic_slice_in_dim(visible, chip_block, 2, 0)
    attended = attend(seen, query_two, windows)
    attended = attended.reshape(4, 2 * tokens, -1)

    straight, switched = [], []
    for along_x, along_z in ((1, 1), (1, 0), (0, 1), (0, 0)):
        wanted = (place_x % 2 ^ along_x) * 2 + (place_z % 2 ^ along_z)
        piece = lax.dynamic_index_in_dim(attended, wanted, 0, keepdims=False)
        if along_x or along_z:
            same = to_mate(piece, along_x, along_z, False)
            other = to_mate(piece, along_x, along_z, True)
        else:
            same, other = piece, crossed(piece)
        here, there = project(core, same, other, rows)
        if along_x or along_z:
            here = from_mate(here, along_x, along_z, False)
            there = from_mate(there, along_x, along_z, True)
        else:
            there = crossed(there)
        straight.append(here.astype(jnp.float32))
        switched.append(there.astype(jnp.float32))
    projected = by_core(first, sum(straight), sum(switched), 1)

    hidden_sum = residual.astype(jnp.float32) + projected
    mean_square = jnp.mean(hidden_sum * hidden_sum, axis=-1, keepdims=True)
    normed = (hidden_sum * lax.rsqrt(mean_square + 1e-05) * norm_gain).astype(jnp.bfloat16)

    mixes, slots = [], []
    for which in range(expert_gate.shape[0]):
        choose = expert_ids == which
        member = jnp.any(choose, axis=1)
        token_weight = jnp.sum(jnp.where(choose, route_weight, 0.0), axis=1)
        ranked = jnp.cumsum(member.astype(jnp.int32)) - member.astype(jnp.int32)
        slot_hit = (ranked[None, :] == jnp.arange(CAP, dtype=jnp.int32)[:, None]) & member[None, :]
        slots.append(slot_hit.astype(jnp.bfloat16))
        mixes.append(jnp.where(slot_hit, token_weight[None, :], 0.0))
    outgoing = jnp.dot(
        jnp.concatenate(slots, axis=0), normed, preferred_element_type=jnp.float32
    ).astype(jnp.bfloat16)

    returned, held = [], outgoing
    for which in range(expert_gate.shape[0]):
        own = held[which * CAP : (which + 1) * CAP]
        pieces = gather_slots(own)
        if which == 0:
            held, pieces[4] = lax.optimization_barrier((held, pieces[4]))
        own_part, other_part = expert(which, pieces, expert_gate, expert_up, expert_down)
        returned.append(return_sums(own_part, other_part))
    expert_mix = jnp.dot(
        jnp.concatenate(mixes, axis=0).T,
        jnp.concatenate(returned, axis=0),
        precision=lax.Precision.HIGHEST,
    )
    return (hidden_sum + expert_mix).astype(jnp.bfloat16)


def solution(mesh):
    finer = Mesh(mesh.devices.reshape(SIZES), AXES)
    in_specs = (
        P(AXES, None),
        P(AXES, None),
        P(AXES, None),
        P(AXES, None),
        P(),
        P(AXES, None),
        P(),
        P(AXES, None),
        P(AXES, None),
        P(None, EP, None),
        P(None, EP, None),
        P(None, EP, None),
    )
    return jax.shard_map(
        local, mesh=finer, in_specs=in_specs, out_specs=P(AXES, None), check_vma=False
    )
```

profile of v0, /device:TPU:0, one launch (start us, length us, event | category | flops | bytes accessed | tf_op | source)
XLA Modules:
  0.0 384.7 jit_solution(10955191958783882163)
XLA Ops:
  20.1 8.1 %collective-permute-done.10 = bf16[2,64,2048]{2,1,0:T(8,128)(2,1)S(1)} collective-permute-done((bf16[2,64,2048]{2,1,0:T(8,128)(2,1)S(1)}, bf16[2,64,2048]{2,1,0:T(8,128)(2,1)S(1)}, u32[]{:S(2)}, u32[]{:S(2)}) %collective-permute-start.10) | collective-permute-done | bytes 524320 | tf_op jit(solution)/shard_map/ppermute | solution.py:35
  28.2 12.1 %collective-permute-done.11 = bf16[2,64,2048]{2,1,0:T(8,128)(2,1)S(1)} collective-permute-done((bf16[2,64,2048]{2,1,0:T(8,128)(2,1)S(1)}, bf16[2,64,2048]{2,1,0:T(8,128)(2,1)S(1)}, u32[]{:S(2)}, u32[]{:S(2)}) %collective-permute-start.11) | collective-permute-done | bytes 524320 | tf_op jit(solution)/shard_map/ppermute | solution.py:35
  48.2 5.7 %collective-permute-start.2 = (bf16[256,1024]{1,0:T(8,128)(2,1)}, bf16[256,1024]{1,0:T(8,128)(2,1)}, u32[]{:S(2)}, u32[]{:S(2)}) collective-permute-start(bf16[256,1024]{1,0:T(8,128)(2,1)} %maximum_select_fusion.2.refs_4_.refs_9_), channel_id=1, source_target_pairs={{0,8},{1,9},{2,10},{3,11},{4,12},{5,13},{6,14},{7,15},{8,16},{9,17... | collective-permute-start | bytes 1572872 | tf_op jit(solution)/shard_map/ppermute | solution.py:68
  53.9 6.2 %collective-permute-start.3 = (bf16[256,1024]{1,0:T(8,128)(2,1)}, bf16[256,1024]{1,0:T(8,128)(2,1)}, u32[]{:S(2)}, u32[]{:S(2)}) collective-permute-start(bf16[256,1024]{1,0:T(8,128)(2,1)} %maximum_select_fusion.2.refs_4_.refs_9_), channel_id=1, source_target_pairs={{0,6},{1,7},{2,8},{3,9},{4,10},{5,11},{6,12},{7,13},{8,14},{9,15},... | collective-permute-start | bytes 1572872 | tf_op jit(solution)/shard_map/ppermute | solution.py:68
  69.2 19.0 %collective-permute-done.2.refs_0_.refs_5_ = bf16[256,1024]{1,0:T(8,128)(2,1)} collective-permute-done((bf16[256,1024]{1,0:T(8,128)(2,1)}, bf16[256,1024]{1,0:T(8,128)(2,1)}, u32[]{:S(2)}, u32[]{:S(2)}) %collective-permute-start.2) | collective-permute-done | bytes 524320 | tf_op jit(solution)/shard_map/ppermute | solution.py:68
  88.2 10.4 %collective-permute-done.4.refs_2_.refs_7_ = bf16[256,1024]{1,0:T(8,128)(2,1)} collective-permute-done((bf16[256,1024]{1,0:T(8,128)(2,1)}, bf16[256,1024]{1,0:T(8,128)(2,1)}, u32[]{:S(2)}, u32[]{:S(2)}) %collective-permute-start.4) | collective-permute-done | bytes 524320 | tf_op jit(solution)/shard_map/ppermute | solution.py:68
  98.6 12.5 %attend.1 = bf16[2,2,256,512]{3,2,1,0:T(8,128)(2,1)} custom-call(s32[2,9]{1,0:T(2,128)} %copy.21.seen_ref, bf16[256,2048]{1,0:T(8,128)(2,1)} %maximum_select_fusion.1.query_ref, bf16[256,1024]{1,0:T(8,128)(2,1)} %collective-permute-done.2.refs_0_.refs_5_, bf16[256,1024]{1,0:T(8,128)(2,1)} %collective-permute-done.3.refs_1_.refs_6_, ...), custom_call_target="tpu_custom_call" | custom-call | flops 6000000000 | bytes 6000000 | tf_op jit(solution)/shard_map/attend/pallas_call | solution.py:127
  113.1 21.3 %collective-permute-start.6 = (bf16[256,512]{1,0:T(8,128)(2,1)S(1)}, bf16[256,512]{1,0:T(8,128)(2,1)S(1)}, u32[]{:S(2)}, u32[]{:S(2)}) collective-permute-start(bf16[256,512]{1,0:T(8,128)(2,1)S(1)} %get-tuple-element.51), channel_id=1, source_target_pairs={{0,36},{1,109},{2,38},{3,111},{4,32},{5,105},{6,34},{7,107},{8,44}... | collective-permute-start | bytes 786440 | tf_op jit(solution)/shard_map/ppermute | solution.py:35
  134.4 26.4 %collective-permute-start.15 = (bf16[256,512]{1,0:T(8,128)(2,1)}, bf16[256,512]{1,0:T(8,128)(2,1)S(1)}, u32[]{:S(2)}, u32[]{:S(2)}) collective-permute-start(bf16[256,512]{1,0:T(8,128)(2,1)} %get-tuple-element.54), channel_id=1, source_target_pairs={{0,32},{1,97},{2,34},{3,99},{4,36},{5,101},{6,38},{7,103},{8,40},{... | collective-permute-start | bytes 786440 | tf_op jit(solution)/shard_map/ppermute | solution.py:35
  173.7 4.9 %project.4 = (bf16[128,2048]{1,0:T(8,128)(2,1)}, bf16[128,2048]{1,0:T(8,128)(2,1)}) custom-call(s32[1]{0:T(128)} %bitcast.core_ref, bf16[2,128,512]{2,1,0:T(8,128)(2,1)} %bitcast.57, bf16[2,128,512]{2,1,0:T(8,128)(2,1)} %bitcast.58, bf16[2,128,512]{2,1,0:T(8,128)(2,1)} %bitcast.59, bf16[2,128,512]{2,1,0:T(8,128)(2,1)} %bitcast.60, ...), custom_call_target="tpu_custom_call" | custom-call | flops 1073741824 | bytes 6000000 | tf_op jit(solution)/shard_map/project/pallas_call | solution.py:172
  179.4 4.9 %project.5 = (bf16[128,2048]{1,0:T(8,128)(2,1)}, bf16[128,2048]{1,0:T(8,128)(2,1)}) custom-call(s32[1]{0:T(128)} %bitcast.core_ref, bf16[2,128,512]{2,1,0:T(8,128)(2,1)} %bitcast.47, bf16[2,128,512]{2,1,0:T(8,128)(2,1)} %bitcast.48, bf16[2,128,512]{2,1,0:T(8,128)(2,1)} %bitcast.51, bf16[2,128,512]{2,1,0:T(8,128)(2,1)} %bitcast.52, ...), custom_call_target="tpu_custom_call" | custom-call | flops 1073741824 | bytes 6000000 | tf_op jit(solution)/shard_map/project/pallas_call | solution.py:172
  187.1 4.9 %project.6 = (bf16[128,2048]{1,0:T(8,128)(2,1)}, bf16[128,2048]{1,0:T(8,128)(2,1)}) custom-call(s32[1]{0:T(128)} %bitcast.core_ref, bf16[2,128,512]{2,1,0:T(8,128)(2,1)} %bitcast.49, bf16[2,128,512]{2,1,0:T(8,128)(2,1)} %bitcast.50, bf16[2,128,512]{2,1,0:T(8,128)(2,1)} %bitcast.55, bf16[2,128,512]{2,1,0:T(8,128)(2,1)} %bitcast.56, ...), custom_call_target="tpu_custom_call" | custom-call | flops 1073741824 | bytes 6000000 | tf_op jit(solution)/shard_map/project/pallas_call | solution.py:172
  194.8 4.9 %project.7 = (bf16[128,2048]{1,0:T(8,128)(2,1)}, bf16[128,2048]{1,0:T(8,128)(2,1)}) custom-call(s32[1]{0:T(128)} %bitcast.core_ref, bf16[2,128,512]{2,1,0:T(8,128)(2,1)} %bitcast.44, bf16[2,128,512]{2,1,0:T(8,128)(2,1)} %bitcast.45, bf16[2,128,512]{2,1,0:T(8,128)(2,1)} %bitcast.53, bf16[2,128,512]{2,1,0:T(8,128)(2,1)} %bitcast.54, ...), custom_call_target="tpu_custom_call" | custom-call | flops 1073741824 | bytes 6000000 | tf_op jit(solution)/shard_map/project/pallas_call | solution.py:172
  211.8 5.3 %collective-permute-done.17 = bf16[128,2048]{1,0:T(8,128)(2,1)S(1)} collective-permute-done((bf16[128,2048]{1,0:T(8,128)(2,1)}, bf16[128,2048]{1,0:T(8,128)(2,1)S(1)}, u32[]{:S(2)}, u32[]{:S(2)}) %collective-permute-start.17) | collective-permute-done | bytes 524320 | tf_op jit(solution)/shard_map/ppermute | solution.py:35
  224.5 6.4 %collective-permute-done.29.refs_4_ = bf16[40,4096]{1,0:T(8,128)(2,1)S(1)} collective-permute-done((bf16[40,4096]{1,0:T(8,128)(2,1)S(1)}, bf16[40,4096]{1,0:T(8,128)(2,1)S(1)}, u32[]{:S(2)}, u32[]{:S(2)}) %collective-permute-start.29) | collective-permute-done | bytes 327712 | tf_op jit(solution)/shard_map/ppermute | solution.py:35
  240.0 5.4 %collective-permute-done.30.refs_5_ = bf16[40,4096]{1,0:T(8,128)(2,1)S(1)} collective-permute-done((bf16[40,4096]{1,0:T(8,128)(2,1)S(1)}, bf16[40,4096]{1,0:T(8,128)(2,1)S(1)}, u32[]{:S(2)}, u32[]{:S(2)}) %collective-permute-start.30) | collective-permute-done | bytes 327712 | tf_op jit(solution)/shard_map/ppermute | solution.py:35
  258.5 5.1 %collective-permute-done.50.refs_2_ = bf16[40,4096]{1,0:T(8,128)(2,1)S(1)} collective-permute-done((bf16[40,4096]{1,0:T(8,128)(2,1)S(1)}, bf16[40,4096]{1,0:T(8,128)(2,1)S(1)}, u32[]{:S(2)}, u32[]{:S(2)}) %collective-permute-start.50) | collective-permute-done | bytes 327712 | tf_op jit(solution)/shard_map/ppermute | solution.py:35
  273.1 6.9 %collective-permute-done.53.refs_5_ = bf16[40,4096]{1,0:T(8,128)(2,1)} collective-permute-done((bf16[40,4096]{1,0:T(8,128)(2,1)}, bf16[40,4096]{1,0:T(8,128)(2,1)}, u32[]{:S(2)}, u32[]{:S(2)}) %collective-permute-start.53) | collective-permute-done | bytes 327712 | tf_op jit(solution)/shard_map/ppermute | solution.py:35
  280.8 8.9 %collective-permute-start.62 = (bf16[40,4096]{1,0:T(8,128)(2,1)}, bf16[40,4096]{1,0:T(8,128)(2,1)}, u32[]{:S(2)}, u32[]{:S(2)}) collective-permute-start(bf16[40,4096]{1,0:T(8,128)(2,1)} %collective-permute-done.54.refs_6_), channel_id=1, source_target_pairs={{0,1},{1,0},{2,3},{3,2},{4,5},{5,4},{6,7},{7,6},{8,9},{9,8},{10,11... | collective-permute-start | bytes 983048 | tf_op jit(solution)/shard_map/ppermute | solution.py:35
  290.8 16.0 %expert.2 = (bf16[320,4096]{1,0:T(8,128)(2,1)}, bf16[320,4096]{1,0:T(8,128)(2,1)}) custom-call(bf16[40,4096]{1,0:T(8,128)(2,1)} %copy-done.4, bf16[40,4096]{1,0:T(8,128)(2,1)} %copy-done.18, bf16[40,4096]{1,0:T(8,128)(2,1)} %copy-done.17, bf16[40,4096]{1,0:T(8,128)(2,1)} %copy-done.19, bf16[40,4096]{1,0:T(8,128)(2,1)} %copy-done.16, ...), custom_call_target="tpu_custom_call" | custom-call | flops 7000000000 | bytes 22000000 | tf_op jit(solution)/shard_map/expert/pallas_call | solution.py:240
  307.1 16.0 %expert.3 = (bf16[320,4096]{1,0:T(8,128)(2,1)}, bf16[320,4096]{1,0:T(8,128)(2,1)}) custom-call(bf16[40,4096]{1,0:T(8,128)(2,1)} %copy-done.5, bf16[40,4096]{1,0:T(8,128)(2,1)} %copy-done.27, bf16[40,4096]{1,0:T(8,128)(2,1)} %copy-done.26, bf16[40,4096]{1,0:T(8,128)(2,1)} %collective-permute-done.51.refs_3_, ...), custom_call_target="tpu_custom_call" | custom-call | flops 7000000000 | bytes 22000000 | tf_op jit(solution)/shard_map/expert/pallas_call | solution.py:240
  345.5 5.0 %collective-permute-done.67 = bf16[40,4096]{1,0:T(8,128)(2,1)S(1)} collective-permute-done((bf16[40,4096]{1,0:T(8,128)(2,1)S(1)}, bf16[40,4096]{1,0:T(8,128)(2,1)S(1)}, u32[]{:S(2)}, u32[]{:S(2)}) %collective-permute-start.67) | collective-permute-done | bytes 327712 | tf_op jit(solution)/shard_map/ppermute | solution.py:35
  359.1 7.1 %collective-permute-done.46 = bf16[40,4096]{1,0:T(8,128)(2,1)S(1)} collective-permute-done((bf16[40,4096]{1,0:T(8,128)(2,1)S(1)}, bf16[40,4096]{1,0:T(8,128)(2,1)S(1)}, u32[]{:S(2)}, u32[]{:S(2)}) %collective-permute-start.46) | collective-permute-done | bytes 327712 | tf_op jit(solution)/shard_map/ppermute | solution.py:35
  376.2 5.0 %collective-permute-done.71 = bf16[40,4096]{1,0:T(8,128)(2,1)S(1)} collective-permute-done((bf16[40,4096]{1,0:T(8,128)(2,1)S(1)}, bf16[40,4096]{1,0:T(8,128)(2,1)S(1)}, u32[]{:S(2)}, u32[]{:S(2)}) %collective-permute-start.71) | collective-permute-done | bytes 327712 | tf_op jit(solution)/shard_map/ppermute | solution.py:35
  (261 shorter events, 155.4 us)
Async XLA Ops:
  8.6 53.6 %collective-permute-start = (bf16[128,2048]{1,0:T(8,128)(2,1)}, bf16[128,2048]{1,0:T(8,128)(2,1)S(1)}, u32[]{:S(2)}, u32[]{:S(2)}) collective-permute-start(bf16[128,2048]{1,0:T(8,128)(2,1)} %get-tuple-element.56), channel_id=1, source_target_pairs={{0,1},{1,0},{2,3},{3,2},{4,5},{5,4},{6,7},{7,6},{8,9},{9,8},{10,11... | collective-permute-start | bytes 1572872 | tf_op jit(solution)/shard_map/ppermute | solution.py:35
  15.5 24.8 %collective-permute-start.11 = (bf16[2,64,2048]{2,1,0:T(8,128)(2,1)S(1)}, bf16[2,64,2048]{2,1,0:T(8,128)(2,1)S(1)}, u32[]{:S(2)}, u32[]{:S(2)}) collective-permute-start(bf16[2,64,2048]{2,1,0:T(8,128)(2,1)S(1)} %bitcast_dynamic-update-slice_fusion.5), channel_id=1, source_target_pairs={{0,2},{1,3},{2,0},{3,1},{4,6},{5,7},{6,4},{7,5},{8,10},{9,11},{10,... | collective-permute-start | bytes 1572872 | tf_op jit(solution)/shard_map/ppermute | solution.py:35
  18.4 22.1 %collective-permute-start.12 = (bf16[2,64,2048]{2,1,0:T(8,128)(2,1)S(1)}, bf16[2,64,2048]{2,1,0:T(8,128)(2,1)S(1)}, u32[]{:S(2)}, u32[]{:S(2)}) collective-permute-start(bf16[2,64,2048]{2,1,0:T(8,128)(2,1)S(1)} %bitcast_dynamic-update-slice_fusion.5), channel_id=1, source_target_pairs={{0,18},{1,19},{2,16},{3,17},{4,22},{5,23},{6,20},{7,21},{8,26},{9,... | collective-permute-start | bytes 1572872 | tf_op jit(solution)/shard_map/ppermute | solution.py:35
  40.7 126.4 %collective-permute-start.13 = (bf16[512,2048]{1,0:T(8,128)(2,1)S(1)}, bf16[512,2048]{1,0:T(8,128)(2,1)}, u32[]{:S(2)}, u32[]{:S(2)}) collective-permute-start(bf16[512,2048]{1,0:T(8,128)(2,1)S(1)} %bitcast.40), channel_id=1, source_target_pairs={{0,64},{1,65},{2,66},{3,67},{4,68},{5,69},{6,70},{7,71},{8,72},{9,... | collective-permute-start | bytes 6291464 | tf_op jit(solution)/shard_map/ppermute | solution.py:35
  48.2 40.0 %collective-permute-start.2 = (bf16[256,1024]{1,0:T(8,128)(2,1)}, bf16[256,1024]{1,0:T(8,128)(2,1)}, u32[]{:S(2)}, u32[]{:S(2)}) collective-permute-start(bf16[256,1024]{1,0:T(8,128)(2,1)} %maximum_select_fusion.2.refs_4_.refs_9_), channel_id=1, source_target_pairs={{0,8},{1,9},{2,10},{3,11},{4,12},{5,13},{6,14},{7,15},{8,16},{9,17... | collective-permute-start | bytes 1572872 | tf_op jit(solution)/shard_map/ppermute | solution.py:68
  53.9 34.3 %collective-permute-start.3 = (bf16[256,1024]{1,0:T(8,128)(2,1)}, bf16[256,1024]{1,0:T(8,128)(2,1)}, u32[]{:S(2)}, u32[]{:S(2)}) collective-permute-start(bf16[256,1024]{1,0:T(8,128)(2,1)} %maximum_select_fusion.2.refs_4_.refs_9_), channel_id=1, source_target_pairs={{0,6},{1,7},{2,8},{3,9},{4,10},{5,11},{6,12},{7,13},{8,14},{9,15},... | collective-permute-start | bytes 1572872 | tf_op jit(solution)/shard_map/ppermute | solution.py:68
  60.1 38.5 %collective-permute-start.4 = (bf16[256,1024]{1,0:T(8,128)(2,1)}, bf16[256,1024]{1,0:T(8,128)(2,1)}, u32[]{:S(2)}, u32[]{:S(2)}) collective-permute-start(bf16[256,1024]{1,0:T(8,128)(2,1)} %maximum_select_fusion.2.refs_4_.refs_9_), channel_id=1, source_target_pairs={{0,4},{1,5},{2,6},{3,7},{4,8},{5,9},{6,10},{7,11},{8,12},{9,13},{1... | collective-permute-start | bytes 1572872 | tf_op jit(solution)/shard_map/ppermute | solution.py:68
  62.2 36.4 %collective-permute-start.5 = (bf16[256,1024]{1,0:T(8,128)(2,1)}, bf16[256,1024]{1,0:T(8,128)(2,1)}, u32[]{:S(2)}, u32[]{:S(2)}) collective-permute-start(bf16[256,1024]{1,0:T(8,128)(2,1)} %maximum_select_fusion.2.refs_4_.refs_9_), channel_id=1, source_target_pairs={{0,2},{1,3},{2,4},{3,5},{4,6},{5,7},{6,8},{7,9},{8,10},{9,11},{10,... | collective-permute-start | bytes 1572872 | tf_op jit(solution)/shard_map/ppermute | solution.py:68
  113.1 54.0 %collective-permute-start.6 = (bf16[256,512]{1,0:T(8,128)(2,1)S(1)}, bf16[256,512]{1,0:T(8,128)(2,1)S(1)}, u32[]{:S(2)}, u32[]{:S(2)}) collective-permute-start(bf16[256,512]{1,0:T(8,128)(2,1)S(1)} %get-tuple-element.51), channel_id=1, source_target_pairs={{0,36},{1,109},{2,38},{3,111},{4,32},{5,105},{6,34},{7,107},{8,44}... | collective-permute-start | bytes 786440 | tf_op jit(solution)/shard_map/ppermute | solution.py:35
  134.3 38.6 %collective-permute-start.7 = (bf16[256,512]{1,0:T(8,128)(2,1)S(1)}, bf16[256,512]{1,0:T(8,128)(2,1)S(1)}, u32[]{:S(2)}, u32[]{:S(2)}) collective-permute-start(bf16[256,512]{1,0:T(8,128)(2,1)S(1)} %get-tuple-element.51), channel_id=1, source_target_pairs={{0,109},{1,36},{2,111},{3,38},{4,105},{5,32},{6,107},{7,34},{8,101... | collective-permute-start | bytes 786440 | tf_op jit(solution)/shard_map/ppermute | solution.py:35
  134.4 44.2 %collective-permute-start.15 = (bf16[256,512]{1,0:T(8,128)(2,1)}, bf16[256,512]{1,0:T(8,128)(2,1)S(1)}, u32[]{:S(2)}, u32[]{:S(2)}) collective-permute-start(bf16[256,512]{1,0:T(8,128)(2,1)} %get-tuple-element.54), channel_id=1, source_target_pairs={{0,32},{1,97},{2,34},{3,99},{4,36},{5,101},{6,38},{7,103},{8,40},{... | collective-permute-start | bytes 786440 | tf_op jit(solution)/shard_map/ppermute | solution.py:35
  167.1 19.2 %collective-permute-start.18 = (bf16[256,512]{1,0:T(8,128)(2,1)S(1)}, bf16[256,512]{1,0:T(8,128)(2,1)S(1)}, u32[]{:S(2)}, u32[]{:S(2)}) collective-permute-start(bf16[256,512]{1,0:T(8,128)(2,1)S(1)} %get-tuple-element.53), channel_id=1, source_target_pairs={{0,4},{1,13},{2,6},{3,15},{4,0},{5,9},{6,2},{7,11},{8,12},{9,5},{1... | collective-permute-start | bytes 786440 | tf_op jit(solution)/shard_map/ppermute | solution.py:35
  167.1 19.2 %collective-permute-start.19 = (bf16[256,512]{1,0:T(8,128)(2,1)S(1)}, bf16[256,512]{1,0:T(8,128)(2,1)S(1)}, u32[]{:S(2)}, u32[]{:S(2)}) collective-permute-start(bf16[256,512]{1,0:T(8,128)(2,1)S(1)} %get-tuple-element.53), channel_id=1, source_target_pairs={{0,13},{1,4},{2,15},{3,6},{4,9},{5,0},{6,11},{7,2},{8,5},{9,12},{1... | collective-permute-start | bytes 786440 | tf_op jit(solution)/shard_map/ppermute | solution.py:35
  173.0 21.1 %collective-permute-start.21 = (bf16[256,512]{1,0:T(8,128)(2,1)S(1)}, bf16[256,512]{1,0:T(8,128)(2,1)S(1)}, u32[]{:S(2)}, u32[]{:S(2)}) collective-permute-start(bf16[256,512]{1,0:T(8,128)(2,1)S(1)} %bitcast.43), channel_id=1, source_target_pairs={{0,1},{1,0},{2,3},{3,2},{4,5},{5,4},{6,7},{7,6},{8,9},{9,8},{10,11... | collective-permute-start | bytes 786440 | tf_op jit(solution)/shard_map/ppermute | solution.py:35
  178.6 23.4 %collective-permute-start.22 = (bf16[128,2048]{1,0:T(8,128)(2,1)}, bf16[128,2048]{1,0:T(8,128)(2,1)S(1)}, u32[]{:S(2)}, u32[]{:S(2)}) collective-permute-start(bf16[128,2048]{1,0:T(8,128)(2,1)} %get-tuple-element.23), channel_id=1, source_target_pairs={{0,37},{1,108},{2,39},{3,110},{4,33},{5,104},{6,35},{7,106},{8,45}... | collective-permute-start | bytes 1572872 | tf_op jit(solution)/shard_map/ppermute | solution.py:35
  184.3 19.9 %collective-permute-start.23 = (bf16[128,2048]{1,0:T(8,128)(2,1)}, bf16[128,2048]{1,0:T(8,128)(2,1)S(1)}, u32[]{:S(2)}, u32[]{:S(2)}) collective-permute-start(bf16[128,2048]{1,0:T(8,128)(2,1)} %get-tuple-element.24), channel_id=1, source_target_pairs={{0,33},{1,96},{2,35},{3,98},{4,37},{5,100},{6,39},{7,102},{8,41},{... | collective-permute-start | bytes 1572872 | tf_op jit(solution)/shard_map/ppermute | solution.py:35
  280.1 27.0 %collective-permute-start.60 = (bf16[40,4096]{1,0:T(8,128)(2,1)}, bf16[40,4096]{1,0:T(8,128)(2,1)}, u32[]{:S(2)}, u32[]{:S(2)}) collective-permute-start(bf16[40,4096]{1,0:T(8,128)(2,1)} %collective-permute-done.52.refs_4_), channel_id=1, source_target_pairs={{0,1},{1,0},{2,3},{3,2},{4,5},{5,4},{6,7},{7,6},{8,9},{9,8},{10,11... | collective-permute-start | bytes 983048 | tf_op jit(solution)/shard_map/ppermute | solution.py:35
  280.3 26.5 %collective-permute-start.59 = (bf16[40,4096]{1,0:T(8,128)(2,1)}, bf16[40,4096]{1,0:T(8,128)(2,1)}, u32[]{:S(2)}, u32[]{:S(2)}) collective-permute-start(bf16[40,4096]{1,0:T(8,128)(2,1)} %collective-permute-done.51.refs_3_), channel_id=1, source_target_pairs={{0,1},{1,0},{2,3},{3,2},{4,5},{5,4},{6,7},{7,6},{8,9},{9,8},{10,11... | collective-permute-start | bytes 983048 | tf_op jit(solution)/shard_map/ppermute | solution.py:35
  280.6 26.5 %collective-permute-start.61 = (bf16[40,4096]{1,0:T(8,128)(2,1)}, bf16[40,4096]{1,0:T(8,128)(2,1)}, u32[]{:S(2)}, u32[]{:S(2)}) collective-permute-start(bf16[40,4096]{1,0:T(8,128)(2,1)} %collective-permute-done.53.refs_5_), channel_id=1, source_target_pairs={{0,1},{1,0},{2,3},{3,2},{4,5},{5,4},{6,7},{7,6},{8,9},{9,8},{10,11... | collective-permute-start | bytes 983048 | tf_op jit(solution)/shard_map/ppermute | solution.py:35
  280.8 26.3 %collective-permute-start.62 = (bf16[40,4096]{1,0:T(8,128)(2,1)}, bf16[40,4096]{1,0:T(8,128)(2,1)}, u32[]{:S(2)}, u32[]{:S(2)}) collective-permute-start(bf16[40,4096]{1,0:T(8,128)(2,1)} %collective-permute-done.54.refs_6_), channel_id=1, source_target_pairs={{0,1},{1,0},{2,3},{3,2},{4,5},{5,4},{6,7},{7,6},{8,9},{9,8},{10,11... | collective-permute-start | bytes 983048 | tf_op jit(solution)/shard_map/ppermute | solution.py:35
  332.0 25.4 %collective-permute-start.42 = (bf16[40,4096]{1,0:T(8,128)(2,1)S(1)}, bf16[40,4096]{1,0:T(8,128)(2,1)S(1)}, u32[]{:S(2)}, u32[]{:S(2)}) collective-permute-start(bf16[40,4096]{1,0:T(8,128)(2,1)S(1)} %get-tuple-element.37), channel_id=1, source_target_pairs={{0,12},{1,13},{2,14},{3,15},{4,0},{5,1},{6,2},{7,3},{8,4},{9,5},{1... | collective-permute-start | bytes 983048 | tf_op jit(solution)/shard_map/ppermute | solution.py:35
  335.3 23.3 %collective-permute-start.43 = (bf16[40,4096]{1,0:T(8,128)(2,1)S(1)}, bf16[40,4096]{1,0:T(8,128)(2,1)S(1)}, u32[]{:S(2)}, u32[]{:S(2)}) collective-permute-start(bf16[40,4096]{1,0:T(8,128)(2,1)S(1)} %get-tuple-element.41), channel_id=1, source_target_pairs={{0,4},{1,5},{2,6},{3,7},{4,8},{5,9},{6,10},{7,11},{8,12},{9,13},{1... | collective-permute-start | bytes 983048 | tf_op jit(solution)/shard_map/ppermute | solution.py:35
  350.5 24.3 %collective-permute-start.65 = (bf16[40,4096]{1,0:T(8,128)(2,1)S(1)}, bf16[40,4096]{1,0:T(8,128)(2,1)S(1)}, u32[]{:S(2)}, u32[]{:S(2)}) collective-permute-start(bf16[40,4096]{1,0:T(8,128)(2,1)S(1)} %get-tuple-element.44), channel_id=1, source_target_pairs={{0,12},{1,13},{2,14},{3,15},{4,0},{5,1},{6,2},{7,3},{8,4},{9,5},{1... | collective-permute-start | bytes 983048 | tf_op jit(solution)/shard_map/ppermute | solution.py:35
  357.4 18.7 %collective-permute-start.66 = (bf16[40,4096]{1,0:T(8,128)(2,1)S(1)}, bf16[40,4096]{1,0:T(8,128)(2,1)S(1)}, u32[]{:S(2)}, u32[]{:S(2)}) collective-permute-start(bf16[40,4096]{1,0:T(8,128)(2,1)S(1)} %get-tuple-element.48), channel_id=1, source_target_pairs={{0,4},{1,5},{2,6},{3,7},{4,8},{5,9},{6,10},{7,11},{8,12},{9,13},{1... | collective-permute-start | bytes 983048 | tf_op jit(solution)/shard_map/ppermute | solution.py:35
  (90 other events, 1475.7 us)
where the time goes:
time: 390 us; the launch traced here: 385 us
  starting transfers between devices  151 us (39%)
  waiting for transfers between devices  131 us (34%)
  Pallas kernels  64.1 us (16%)
  local copies, waits for them, and re-layouts  19.7 us (5%)
  other arithmetic  13.8 us (4%)
    ppermute x68, starting transfers between devices, sent(): return lax.ppermute(value, AXES, pairs)  133 us
    ppermute x68, waiting for transfers between devices, sent(): return lax.ppermute(value, AXES, pairs)  102 us
    pallas_call x2, Pallas kernels, expert(): pl.pallas_call(expert_kernel, grid=(8,), in_specs=[*[pl.BlockSpec((slots,...  31.9 us
    ppermute x4, waiting for transfers between devices, later(): lax.ppermute(value, AXES, [(s, s + blocks) for s in range(count - blocks)])  29.4 us
    pallas_call x4, Pallas kernels, project(): pl.pallas_call(project_kernel, grid_spec=pltpu.PrefetchScalarGridSpec(num...  19.6 us
    ppermute x4, starting transfers between devices, later(): lax.ppermute(value, AXES, [(s, s + blocks) for s in range(count - blocks)])  17.9 us
    pallas_call x1, Pallas kernels, attend(): pl.pallas_call(attend_kernel, grid=(4,), in_specs=[pl.BlockSpec(memory_sp...  12.5 us
  transfers between devices with their start and end apart: 72, of which 27 were waited for; matrix products, arithmetic and copies ran while one was open for 7% of the time, Pallas kernels for 17%

commit v1 on v0

--- a/solution.py
+++ b/solution.py
@@ -7,6 +7,7 @@
 from jax.experimental.pallas import tpu as pltpu
 from jax.sharding import Mesh
 from jax.sharding import PartitionSpec as P
+
 
 HEAD = 128
 CAP = 40
@@ -151,20 +152,20 @@
 
 
 def project_kernel(core_ref, *refs):
-    mine, mine_other, theirs, theirs_other, rows_own, rows_other, straight_ref, switch_ref = refs
-    left = jnp.concatenate([mine[0], mine_other[0]], axis=0)
-    right = jnp.concatenate([theirs[0], theirs_other[0]], axis=0)
+    same, other, (rows_own, rows_other) = refs[:8], refs[8:16], refs[16:18]
+    left = jnp.concatenate([ref[0] for ref in same], axis=0)
+    right = jnp.concatenate([ref[0] for ref in other], axis=0)
     product = jnp.dot(left, rows_own[0], preferred_element_type=jnp.float32)
     product += jnp.dot(right, rows_other[0], preferred_element_type=jnp.float32)
     product = product.astype(jnp.bfloat16)
-    straight_ref[...] = product[:128]
-    switch_ref[...] = product[128:]
-
-
-def project(core, own_heads, other_heads, rows):
+    for place, out_ref in enumerate(refs[18:]):
+        out_ref[...] = product[place * 128 : (place + 1) * 128]
+
+
+def project(core, same, other, rows):
     columns = 512
-    own_heads = own_heads.reshape(2, 128, 512)
-    other_heads = other_heads.reshape(2, 128, 512)
+    same = [heads.reshape(2, 128, 512) for heads in same for _ in range(2)]
+    other = [heads.reshape(2, 128, 512) for heads in other for _ in range(2)]
     here = pl.BlockSpec((1, 128, 512), lambda n, core: (core[0], 0, 0))
     there = pl.BlockSpec((1, 128, 512), lambda n, core: (1 - core[0], 0, 0))
     out = pl.BlockSpec((128, columns), lambda n, core: (0, n))
@@ -175,32 +176,29 @@
             num_scalar_prefetch=1,
             grid=(rows.shape[2] // columns,),
             in_specs=[
-                here,
-                there,
-                here,
-                there,
+                *[here, there] * 8,
                 pl.BlockSpec((1, 512, columns), lambda n, core: (core[0], 0, n)),
                 pl.BlockSpec((1, 512, columns), lambda n, core: (1 - core[0], 0, n)),
             ],
-            out_specs=[out, out],
+            out_specs=[out] * 8,
         ),
-        out_shape=[shape, shape],
+        out_shape=[shape] * 8,
         name="project",
         cost_estimate=pl.CostEstimate(
-            flops=1_073_741_824, transcendentals=0, bytes_accessed=6_000_000
+            flops=4_300_000_000, transcendentals=0, bytes_accessed=10_000_000
         ),
-    )(core.reshape(1), own_heads, own_heads, other_heads, other_heads, rows, rows)
+    )(core.reshape(1), *same, *other, rows, rows)
 
 
 def expert_kernel(*refs):
-    slot_refs, (gate_ref, up_ref, down_ref, own_ref, other_ref) = refs[:16], refs[16:21]
-    gate_sum, up_sum, act = refs[21:]
-    step = pl.program_id(0)
+    slot_refs, (gate_ref, up_ref, down_ref, own_ref, other_ref) = refs[:4], refs[4:9]
+    gate_sum, up_sum, act = refs[9:]
+    step = pl.program_id(1)
     contract = (((1,), (1,)), ((), ()))
 
     @pl.when(step < 4)
     def _():
-        slots = jnp.concatenate([ref[...] for ref in slot_refs], axis=0)
+        slots = jnp.concatenate([ref[0] for ref in slot_refs], axis=0)
         gate = lax.dot_general(slots, gate_ref[0], contract, preferred_element_type=jnp.float32)
         up = lax.dot_general(slots, up_ref[0], contract, preferred_element_type=jnp.float32)
 
@@ -224,38 +222,38 @@
         result = jnp.dot(act[...], down_ref[0], preferred_element_type=jnp.float32)
         result = result.astype(jnp.bfloat16)
         half = result.shape[0] // 2
-        own_ref[...] = result[:half]
-        other_ref[...] = result[half:]
-
-
-def expert(which, pieces, gate, up, down):
-    slots, width = pieces[0].shape
+        own_ref[0] = result[:half]
+        other_ref[0] = result[half:]
+
+
+def experts(pieces, gate, up, down):
+    count, slots, width = pieces[0].shape
     hidden = gate.shape[1]
     chunk = width // 4
-    count = len(pieces) * slots
-    early = lambda step: jnp.minimum(step, 3)
-    late = lambda step: jnp.maximum(step - 4, 0)
-    out = pl.BlockSpec((count // 2, chunk), lambda step: (0, late(step)))
-    shape = jax.ShapeDtypeStruct((count // 2, width), jnp.bfloat16)
+    rows = len(pieces) * slots
+    early = lambda e, step: (e, 0, jnp.minimum(step, 3))
+    late = lambda e, step: (e, 0, jnp.maximum(step - 4, 0))
+    out = pl.BlockSpec((1, rows // 2, chunk), late)
+    shape = jax.ShapeDtypeStruct((count, rows // 2, width), jnp.bfloat16)
     return pl.pallas_call(
         expert_kernel,
-        grid=(8,),
+        grid=(count, 8),
         in_specs=[
-            *[pl.BlockSpec((slots, chunk), lambda step: (0, early(step))) for _ in pieces],
-            pl.BlockSpec((1, hidden, chunk), lambda step: (which, 0, early(step))),
-            pl.BlockSpec((1, hidden, chunk), lambda step: (which, 0, early(step))),
-            pl.BlockSpec((1, hidden, chunk), lambda step: (which, 0, late(step))),
+            *[pl.BlockSpec((1, slots, chunk), early) for _ in pieces],
+            pl.BlockSpec((1, hidden, chunk), early),
+            pl.BlockSpec((1, hidden, chunk), early),
+            pl.BlockSpec((1, hidden, chunk), late),
         ],
         out_specs=[out, out],
         out_shape=[shape, shape],
         scratch_shapes=[
-            pltpu.VMEM((count, hidden), jnp.float32),
-            pltpu.VMEM((count, hidden), jnp.float32),
-            pltpu.VMEM((count, hidden), jnp.bfloat16),
+            pltpu.VMEM((rows, hidden), jnp.float32),
+            pltpu.VMEM((rows, hidden), jnp.float32),
+            pltpu.VMEM((rows, hidden), jnp.bfloat16),
         ],
-        name="expert",
+        name="experts",
         cost_estimate=pl.CostEstimate(
-            flops=7_000_000_000, transcendentals=300_000, bytes_accessed=22_000_000
+            flops=14_000_000_000, transcendentals=600_000, bytes_accessed=44_000_000
         ),
     )(*pieces, gate, up, down)
 
@@ -266,10 +264,11 @@
 
 def gather_slots(own):
     flip = moved(own, y=2)
-    up1, up3, up2 = moved(own, z=1), moved(own, z=3), moved(own, z=2)
+    up2, up1, up3 = moved(own, z=2), moved(own, z=1), moved(own, z=3)
     flip1, flip3, flip2 = moved(flip, z=1), moved(flip, z=3), moved(up2, y=2)
-    pieces = [own, up1, up2, up3, flip, flip1, flip2, flip3]
-    return pieces + [crossed(piece) for piece in pieces]
+    early = jnp.concatenate([own, up1, up3, flip], axis=1)
+    late = jnp.concatenate([up2, flip1, flip3, flip2], axis=1)
+    return [early, late, crossed(early), crossed(late)]
 
 
 def return_sums(own_part, other_part):
@@ -277,14 +276,15 @@
 
     def owed(place):
         rows = slice(place * CAP, (place + 1) * CAP)
-        return total(own_part[rows], swapped[rows])
-
-    side1, side3 = moved(owed(5), z=3), moved(owed(7), z=1)
-    far = moved(owed(6), y=2)
-    near1, near3 = moved(owed(1), z=3), moved(owed(3), z=1)
-    across = moved(total(owed(4), side1, side3), y=2)
-    twice = moved(total(owed(2), far), z=2)
-    return sum(t.astype(jnp.float32) for t in (owed(0), near1, near3, across, twice))
+        return total(own_part[:, rows], swapped[:, rows])
+
+    own, up1, up3, flip, up2, flip1, flip3, flip2 = [owed(place) for place in range(8)]
+    side1, side3 = moved(flip1, z=3), moved(flip3, z=1)
+    far = moved(flip2, y=2)
+    near1, near3 = moved(up1, z=3), moved(up3, z=1)
+    across = moved(total(flip, side1, side3), y=2)
+    twice = moved(total(up2, far), z=2)
+    return sum(t.astype(jnp.float32) for t in (own, near1, near3, across, twice))
 
 
 def local(
@@ -309,33 +309,41 @@
 
     kv_own = jnp.concatenate([half_of(key_rows, core), half_of(value_rows, core)], axis=1)
     kv_give = jnp.concatenate([half_of(key_rows, 1 - core), half_of(value_rows, 1 - core)], axis=1)
-    kv_two = by_core(first, kv_own, crossed(kv_give), 0)
-    query_two = by_core(first, half_of(queries, core), crossed(half_of(queries, 1 - core)), 0)
+    kv_got = crossed(kv_give)
+    kv_two = by_core(first, kv_own, kv_got, 0)
+    query_got = crossed(half_of(queries, 1 - core))
+    query_two = by_core(first, half_of(queries, core), query_got, 0)
     windows = [later(kv_two, blocks) for blocks in (8, 6, 4, 2)] + [kv_two]
 
     columns = out_proj.shape[1] // 2
-    rows = by_core(first, half_of(out_proj, core), crossed(half_of(out_proj, 1 - core)), 0)
-    rows = in_order([rows, moved(rows, z=2)], place_z // 2)
-    rows = in_order([rows] + [moved(rows, y=step) for step in (1, 2, 3)], place_y)
+    rows_got = crossed(half_of(out_proj, 1 - core))
+    rows = by_core(first, half_of(out_proj, core), rows_got, 0)
+    rows_got = moved(rows, z=2)
+    rows = in_order([rows, rows_got], place_z // 2)
+    rows_got = [moved(rows, y=step) for step in (1, 2, 3)]
+    rows = in_order([rows, *rows_got], place_y)
     rows = rows.reshape(2, 2, 2, 2 * out_proj.shape[0], columns)
     rows = rows.transpose(1, 2, 0, 3, 4).reshape(-1, columns)
-    rows = in_order([rows, moved(rows, x=2)], place_x // 2)
+    rows_got = moved(rows, x=2)
+    rows = in_order([rows, rows_got], place_x // 2)
 
     chip_block = lax.axis_index(AXES) - core
     seen = lax.dynamic_slice_in_dim(visible, chip_block, 2, 0)
     attended = attend(seen, query_two, windows)
     attended = attended.reshape(4, 2 * tokens, -1)
 
-    straight, switched = [], []
-    for along_x, along_z in ((1, 1), (1, 0), (0, 1), (0, 0)):
+    ways = ((1, 1), (1, 0), (0, 1), (0, 0))
+    same, other = [], []
+    for along_x, along_z in ways:
         wanted = (place_x % 2 ^ along_x) * 2 + (place_z % 2 ^ along_z)
         piece = lax.dynamic_index_in_dim(attended, wanted, 0, keepdims=False)
-        if along_x or along_z:
-            same = to_mate(piece, along_x, along_z, False)
-            other = to_mate(piece, along_x, along_z, True)
-        else:
-            same, other = piece, crossed(piece)
-        here, there = project(core, same, other, rows)
+        remote = along_x or along_z
+        same.append(to_mate(piece, along_x, along_z, False) if remote else piece)
+        other.append(to_mate(piece, along_x, along_z, True) if remote else crossed(piece))
+    products = project(core, same, other, rows)
+    straight, switched = [], []
+    for place, (along_x, along_z) in enumerate(ways):
+        here, there = products[2 * place : 2 * place + 2]
         if along_x or along_z:
             here = from_mate(here, along_x, along_z, False)
             there = from_mate(there, along_x, along_z, True)
@@ -362,17 +370,11 @@
         jnp.concatenate(slots, axis=0), normed, preferred_element_type=jnp.float32
     ).astype(jnp.bfloat16)
 
-    returned, held = [], outgoing
-    for which in range(expert_gate.shape[0]):
-        own = held[which * CAP : (which + 1) * CAP]
-        pieces = gather_slots(own)
-        if which == 0:
-            held, pieces[4] = lax.optimization_barrier((held, pieces[4]))
-        own_part, other_part = expert(which, pieces, expert_gate, expert_up, expert_down)
-        returned.append(return_sums(own_part, other_part))
+    pieces = gather_slots(outgoing.reshape(-1, CAP, outgoing.shape[1]))
+    returned = return_sums(*experts(pieces, expert_gate, expert_up, expert_down))
     expert_mix = jnp.dot(
         jnp.concatenate(mixes, axis=0).T,
-        jnp.concatenate(returned, axis=0),
+        returned.reshape(-1, returned.shape[2]),
         precision=lax.Precision.HIGHEST,
     )
     return (hidden_sum + expert_mix).astype(jnp.bfloat16)

time: 390 us -> 368 us (0.944)
  starting transfers between devices: 151 us -> 116 us
  waiting for transfers between devices: 131 us -> 162 us
  Pallas kernels: 64.1 us -> 50.8 us
    ppermute x68 -> x39, starting transfers between devices: 133 us -> 98.5 us  [sent(): return lax.ppermute(value, AXES, pairs)]
    ppermute x68 -> x39, waiting for transfers between devices: 102 us -> 133 us  [sent(): return lax.ppermute(value, AXES, pairs)]
    pallas_call x4 -> x1, Pallas kernels: 19.6 us -> 8.24 us  [project(): pl.pallas_call(project_kernel, grid_spec=pltpu.PrefetchScalarGridSpec(num...]
    pallas_call x2 -> x1, Pallas kernels: 31.9 us -> 30.1 us  [experts(): pl.pallas_call(expert_kernel, grid=(count, 8), in_specs=[*[pl.BlockSpec((...]
  transfers between devices with their start and end apart: 72 -> 43, of which waited for: 27 -> 31; matrix products, arithmetic and copies ran while one was open for 7% -> 6% of each run, Pallas kernels for 17% -> 3%
where the time goes in v1:
time: 368 us; the launch traced here: 366 us
  waiting for transfers between devices  162 us (44%)
  starting transfers between devices  116 us (32%)
  Pallas kernels  50.8 us (14%)
  local copies, waits for them, and re-layouts  18.4 us (5%)
  other arithmetic  13.3 us (4%)
  matrix products  3.78 us (1%)
    ppermute x39, waiting for transfers between devices, sent(): return lax.ppermute(value, AXES, pairs)  133 us
    ppermute x39, starting transfers between devices, sent(): return lax.ppermute(value, AXES, pairs)  98.5 us
    pallas_call x1, Pallas kernels, experts(): pl.pallas_call(expert_kernel, grid=(count, 8), in_specs=[*[pl.BlockSpec((...  30.1 us
    ppermute x4, waiting for transfers between devices, later(): lax.ppermute(value, AXES, [(s, s + blocks) for s in range(count - blocks)])  29.5 us
    ppermute x4, starting transfers between devices, later(): lax.ppermute(value, AXES, [(s, s + blocks) for s in range(count - blocks)])  17.9 us
    pallas_call x1, Pallas kernels, attend(): pl.pallas_call(attend_kernel, grid=(4,), in_specs=[pl.BlockSpec(memory_sp...  12.5 us
    pallas_call x1, Pallas kernels, project(): pl.pallas_call(project_kernel, grid_spec=pltpu.PrefetchScalarGridSpec(num...  8.24 us
  transfers between devices with their start and end apart: 43, of which 31 were waited for; matrix products, arithmetic and copies ran while one was open for 6% of the time, Pallas kernels for 3%

profile of v1, /device:TPU:0, one launch (start us, length us, event | category | flops | bytes accessed | tf_op | source)
XLA Modules:
  0.0 365.7 jit_solution(429657675853078034)
XLA Ops:
  2.5 4.1 %collective-permute-start.14 = (bf16[64,2048]{1,0:T(8,128)(2,1)S(1)}, bf16[64,2048]{1,0:T(8,128)(2,1)S(1)}, u32[]{:S(2)}, u32[]{:S(2)}) collective-permute-start(bf16[64,2048]{1,0:T(8,128)(2,1)S(1)} %maximum_select_fusion.4), channel_id=1, source_target_pairs={{0,8},{1,9},{2,10},{3,11},{4,12},{5,13},{6,14},{7,15},{8,0},{9,1},... | collective-permute-start | bytes 786440 | tf_op jit(solution)/shard_map/ppermute | solution.py:36
  8.7 4.4 %collective-permute-done.14 = bf16[64,2048]{1,0:T(8,128)(2,1)S(1)} collective-permute-done((bf16[64,2048]{1,0:T(8,128)(2,1)S(1)}, bf16[64,2048]{1,0:T(8,128)(2,1)S(1)}, u32[]{:S(2)}, u32[]{:S(2)}) %collective-permute-start.14) | collective-permute-done | bytes 262176 | tf_op jit(solution)/shard_map/ppermute | solution.py:36
  20.1 8.1 %collective-permute-done.15 = bf16[2,64,2048]{2,1,0:T(8,128)(2,1)S(1)} collective-permute-done((bf16[2,64,2048]{2,1,0:T(8,128)(2,1)S(1)}, bf16[2,64,2048]{2,1,0:T(8,128)(2,1)S(1)}, u32[]{:S(2)}, u32[]{:S(2)}) %collective-permute-start.15) | collective-permute-done | bytes 524320 | tf_op jit(solution)/shard_map/ppermute | solution.py:36
  28.2 12.1 %collective-permute-done.16 = bf16[2,64,2048]{2,1,0:T(8,128)(2,1)S(1)} collective-permute-done((bf16[2,64,2048]{2,1,0:T(8,128)(2,1)S(1)}, bf16[2,64,2048]{2,1,0:T(8,128)(2,1)S(1)}, u32[]{:S(2)}, u32[]{:S(2)}) %collective-permute-start.16) | collective-permute-done | bytes 524320 | tf_op jit(solution)/shard_map/ppermute | solution.py:36
  48.3 5.7 %collective-permute-start.2 = (bf16[256,1024]{1,0:T(8,128)(2,1)}, bf16[256,1024]{1,0:T(8,128)(2,1)}, u32[]{:S(2)}, u32[]{:S(2)}) collective-permute-start(bf16[256,1024]{1,0:T(8,128)(2,1)} %maximum_select_fusion.2.refs_4_.refs_9_), channel_id=1, source_target_pairs={{0,8},{1,9},{2,10},{3,11},{4,12},{5,13},{6,14},{7,15},{8,16},{9,17... | collective-permute-start | bytes 1572872 | tf_op jit(solution)/shard_map/ppermute | solution.py:69
  53.9 6.3 %collective-permute-start.3 = (bf16[256,1024]{1,0:T(8,128)(2,1)}, bf16[256,1024]{1,0:T(8,128)(2,1)}, u32[]{:S(2)}, u32[]{:S(2)}) collective-permute-start(bf16[256,1024]{1,0:T(8,128)(2,1)} %maximum_select_fusion.2.refs_4_.refs_9_), channel_id=1, source_target_pairs={{0,6},{1,7},{2,8},{3,9},{4,10},{5,11},{6,12},{7,13},{8,14},{9,15},... | collective-permute-start | bytes 1572872 | tf_op jit(solution)/shard_map/ppermute | solution.py:69
  69.1 19.1 %collective-permute-done.2.refs_0_.refs_5_ = bf16[256,1024]{1,0:T(8,128)(2,1)} collective-permute-done((bf16[256,1024]{1,0:T(8,128)(2,1)}, bf16[256,1024]{1,0:T(8,128)(2,1)}, u32[]{:S(2)}, u32[]{:S(2)}) %collective-permute-start.2) | collective-permute-done | bytes 524320 | tf_op jit(solution)/shard_map/ppermute | solution.py:69
  88.2 10.4 %collective-permute-done.4.refs_2_.refs_7_ = bf16[256,1024]{1,0:T(8,128)(2,1)} collective-permute-done((bf16[256,1024]{1,0:T(8,128)(2,1)}, bf16[256,1024]{1,0:T(8,128)(2,1)}, u32[]{:S(2)}, u32[]{:S(2)}) %collective-permute-start.4) | collective-permute-done | bytes 524320 | tf_op jit(solution)/shard_map/ppermute | solution.py:69
  98.7 12.5 %attend.1 = bf16[2,2,256,512]{3,2,1,0:T(8,128)(2,1)} custom-call(s32[2,9]{1,0:T(2,128)} %copy.21.seen_ref, bf16[256,2048]{1,0:T(8,128)(2,1)} %maximum_select_fusion.1.query_ref, bf16[256,1024]{1,0:T(8,128)(2,1)} %collective-permute-done.2.refs_0_.refs_5_, bf16[256,1024]{1,0:T(8,128)(2,1)} %collective-permute-done.3.refs_1_.refs_6_, ...), custom_call_target="tpu_custom_call" | custom-call | flops 6000000000 | bytes 6000000 | tf_op jit(solution)/shard_map/attend/pallas_call | solution.py:128
  112.4 46.1 %collective-permute-start.10 = (bf16[256,512]{1,0:T(8,128)(2,1)S(1)}, bf16[256,512]{1,0:T(8,128)(2,1)S(1)}, u32[]{:S(2)}, u32[]{:S(2)}) collective-permute-start(bf16[256,512]{1,0:T(8,128)(2,1)S(1)} %get-tuple-element.38), channel_id=1, source_target_pairs={{0,97},{1,32},{2,99},{3,34},{4,101},{5,36},{6,103},{7,38},{8,105},... | collective-permute-start | bytes 786440 | tf_op jit(solution)/shard_map/ppermute | solution.py:36
  166.5 4.9 %collective-permute-start.9 = (bf16[256,512]{1,0:T(8,128)(2,1)S(1)}, bf16[256,512]{1,0:T(8,128)(2,1)S(1)}, u32[]{:S(2)}, u32[]{:S(2)}) collective-permute-start(bf16[256,512]{1,0:T(8,128)(2,1)S(1)} %get-tuple-element.39), channel_id=1, source_target_pairs={{0,109},{1,36},{2,111},{3,38},{4,105},{5,32},{6,107},{7,34},{8,101... | collective-permute-start | bytes 786440 | tf_op jit(solution)/shard_map/ppermute | solution.py:36
  176.1 8.2 %project.1 = (bf16[128,2048]{1,0:T(8,128)(2,1)}, bf16[128,2048]{1,0:T(8,128)(2,1)}, bf16[128,2048]{1,0:T(8,128)(2,1)}, bf16[128,2048]{1,0:T(8,128)(2,1)}, bf16[1...) custom-call(s32[1]{0:T(128)} %bitcast.core_ref, ...), custom_call_target="tpu_custom_call" | custom-call | flops 4300000256 | bytes 10000000 | tf_op jit(solution)/shard_map/project/pallas_call | solution.py:173
  184.4 5.5 %collective-permute-start.23 = (bf16[128,2048]{1,0:T(8,128)(2,1)}, bf16[128,2048]{1,0:T(8,128)(2,1)S(1)}, u32[]{:S(2)}, u32[]{:S(2)}) collective-permute-start(bf16[128,2048]{1,0:T(8,128)(2,1)} %get-tuple-element.20), channel_id=1, source_target_pairs={{0,33},{1,96},{2,35},{3,98},{4,37},{5,100},{6,39},{7,102},{8,41},{... | collective-permute-start | bytes 1572872 | tf_op jit(solution)/shard_map/ppermute | solution.py:36
  191.9 4.7 %collective-permute-done.22 = bf16[128,2048]{1,0:T(8,128)(2,1)S(1)} collective-permute-done((bf16[128,2048]{1,0:T(8,128)(2,1)}, bf16[128,2048]{1,0:T(8,128)(2,1)S(1)}, u32[]{:S(2)}, u32[]{:S(2)}) %collective-permute-start.22) | collective-permute-done | bytes 524320 | tf_op jit(solution)/shard_map/ppermute | solution.py:36
  204.3 4.1 %collective-permute-done.19 = bf16[128,2048]{1,0:T(8,128)(2,1)S(1)} collective-permute-done((bf16[128,2048]{1,0:T(8,128)(2,1)}, bf16[128,2048]{1,0:T(8,128)(2,1)S(1)}, u32[]{:S(2)}, u32[]{:S(2)}) %collective-permute-start.19) | collective-permute-done | bytes 524320 | tf_op jit(solution)/shard_map/ppermute | solution.py:36
  219.5 13.7 %collective-permute-done.28 = bf16[2,40,4096]{2,1,0:T(8,128)(2,1)S(1)} collective-permute-done((bf16[2,40,4096]{2,1,0:T(8,128)(2,1)S(1)}, bf16[2,40,4096]{2,1,0:T(8,128)(2,1)S(1)}, u32[]{:S(2)}, u32[]{:S(2)}) %collective-permute-start.28) | collective-permute-done | bytes 655392 | tf_op jit(solution)/shard_map/ppermute | solution.py:36
  235.0 11.1 %collective-permute-done.26 = bf16[2,40,4096]{2,1,0:T(8,128)(2,1)S(1)} collective-permute-done((bf16[2,40,4096]{2,1,0:T(8,128)(2,1)S(1)}, bf16[2,40,4096]{2,1,0:T(8,128)(2,1)S(1)}, u32[]{:S(2)}, u32[]{:S(2)}) %collective-permute-start.26) | collective-permute-done | bytes 655392 | tf_op jit(solution)/shard_map/ppermute | solution.py:36
  252.2 9.0 %collective-permute-done.30 = bf16[2,40,4096]{2,1,0:T(8,128)(2,1)S(1)} collective-permute-done((bf16[2,40,4096]{2,1,0:T(8,128)(2,1)S(1)}, bf16[2,40,4096]{2,1,0:T(8,128)(2,1)S(1)}, u32[]{:S(2)}, u32[]{:S(2)}) %collective-permute-start.30) | collective-permute-done | bytes 655392 | tf_op jit(solution)/shard_map/ppermute | solution.py:36
  272.2 30.1 %experts.1 = (bf16[2,320,4096]{2,1,0:T(8,128)(2,1)}, bf16[2,320,4096]{2,1,0:T(8,128)(2,1)}) custom-call(bf16[2,160,4096]{2,1,0:T(8,128)(2,1)} %copy-done.2, bf16[2,160,4096]{2,1,0:T(8,128)(2,1)} %copy-done.8, bf16[2,160,4096]{2,1,0:T(8,128)(2,1)} %copy-done.12, bf16[2,160,4096]{2,1,0:T(8,128)(2,1)} %collective-permute-done.34.refs_3_, ...), custom_call_target="tpu_custom_call" | custom-call | flops 14000000000 | bytes 44000000 | tf_op jit(solution)/shard_map/experts/pallas_call | solution.py:238
  302.4 8.7 %collective-permute-done.35 = bf16[2,320,4096]{2,1,0:T(8,128)(2,1)S(1)} collective-permute-done((bf16[2,320,4096]{2,1,0:T(8,128)(2,1)}, bf16[2,320,4096]{2,1,0:T(8,128)(2,1)S(1)}, u32[]{:S(2)}, u32[]{:S(2)}) %collective-permute-start.35) | collective-permute-done | bytes 5242912 | tf_op jit(solution)/shard_map/ppermute | solution.py:36
  321.5 10.3 %collective-permute-done.38 = bf16[2,40,4096]{2,1,0:T(8,128)(2,1)S(1)} collective-permute-done((bf16[2,40,4096]{2,1,0:T(8,128)(2,1)S(1)}, bf16[2,40,4096]{2,1,0:T(8,128)(2,1)S(1)}, u32[]{:S(2)}, u32[]{:S(2)}) %collective-permute-start.38) | collective-permute-done | bytes 655392 | tf_op jit(solution)/shard_map/ppermute | solution.py:36
  341.4 4.5 %collective-permute-done.36 = bf16[2,40,4096]{2,1,0:T(8,128)(2,1)S(1)} collective-permute-done((bf16[2,40,4096]{2,1,0:T(8,128)(2,1)S(1)}, bf16[2,40,4096]{2,1,0:T(8,128)(2,1)S(1)}, u32[]{:S(2)}, u32[]{:S(2)}) %collective-permute-start.36) | collective-permute-done | bytes 655392 | tf_op jit(solution)/shard_map/ppermute | solution.py:36
  346.7 6.4 %collective-permute-done.40 = bf16[2,40,4096]{2,1,0:T(8,128)(2,1)S(1)} collective-permute-done((bf16[2,40,4096]{2,1,0:T(8,128)(2,1)S(1)}, bf16[2,40,4096]{2,1,0:T(8,128)(2,1)S(1)}, u32[]{:S(2)}, u32[]{:S(2)}) %collective-permute-start.40) | collective-permute-done | bytes 655392 | tf_op jit(solution)/shard_map/ppermute | solution.py:36
  353.1 7.8 %collective-permute-done.42 = bf16[2,40,4096]{2,1,0:T(8,128)(2,1)S(1)} collective-permute-done((bf16[2,40,4096]{2,1,0:T(8,128)(2,1)S(1)}, bf16[2,40,4096]{2,1,0:T(8,128)(2,1)S(1)}, u32[]{:S(2)}, u32[]{:S(2)}) %collective-permute-start.42) | collective-permute-done | bytes 655392 | tf_op jit(solution)/shard_map/ppermute | solution.py:36
  (157 shorter events, 107.5 us)
Async XLA Ops:
  8.6 53.7 %collective-permute-start = (bf16[128,2048]{1,0:T(8,128)(2,1)}, bf16[128,2048]{1,0:T(8,128)(2,1)S(1)}, u32[]{:S(2)}, u32[]{:S(2)}) collective-permute-start(bf16[128,2048]{1,0:T(8,128)(2,1)} %get-tuple-element.41), channel_id=1, source_target_pairs={{0,1},{1,0},{2,3},{3,2},{4,5},{5,4},{6,7},{7,6},{8,9},{9,8},{10,11... | collective-permute-start | bytes 1572872 | tf_op jit(solution)/shard_map/ppermute | solution.py:36
  15.5 24.8 %collective-permute-start.16 = (bf16[2,64,2048]{2,1,0:T(8,128)(2,1)S(1)}, bf16[2,64,2048]{2,1,0:T(8,128)(2,1)S(1)}, u32[]{:S(2)}, u32[]{:S(2)}) collective-permute-start(bf16[2,64,2048]{2,1,0:T(8,128)(2,1)S(1)} %bitcast_dynamic-update-slice_fusion.5), channel_id=1, source_target_pairs={{0,2},{1,3},{2,0},{3,1},{4,6},{5,7},{6,4},{7,5},{8,10},{9,11},{10,... | collective-permute-start | bytes 1572872 | tf_op jit(solution)/shard_map/ppermute | solution.py:36
  18.4 22.1 %collective-permute-start.17 = (bf16[2,64,2048]{2,1,0:T(8,128)(2,1)S(1)}, bf16[2,64,2048]{2,1,0:T(8,128)(2,1)S(1)}, u32[]{:S(2)}, u32[]{:S(2)}) collective-permute-start(bf16[2,64,2048]{2,1,0:T(8,128)(2,1)S(1)} %bitcast_dynamic-update-slice_fusion.5), channel_id=1, source_target_pairs={{0,18},{1,19},{2,16},{3,17},{4,22},{5,23},{6,20},{7,21},{8,26},{9,... | collective-permute-start | bytes 1572872 | tf_op jit(solution)/shard_map/ppermute | solution.py:36
  40.7 130.6 %collective-permute-start.18 = (bf16[512,2048]{1,0:T(8,128)(2,1)S(1)}, bf16[512,2048]{1,0:T(8,128)(2,1)}, u32[]{:S(2)}, u32[]{:S(2)}) collective-permute-start(bf16[512,2048]{1,0:T(8,128)(2,1)S(1)} %bitcast.43), channel_id=1, source_target_pairs={{0,64},{1,65},{2,66},{3,67},{4,68},{5,69},{6,70},{7,71},{8,72},{9,... | collective-permute-start | bytes 6291464 | tf_op jit(solution)/shard_map/ppermute | solution.py:36
  48.3 40.0 %collective-permute-start.2 = (bf16[256,1024]{1,0:T(8,128)(2,1)}, bf16[256,1024]{1,0:T(8,128)(2,1)}, u32[]{:S(2)}, u32[]{:S(2)}) collective-permute-start(bf16[256,1024]{1,0:T(8,128)(2,1)} %maximum_select_fusion.2.refs_4_.refs_9_), channel_id=1, source_target_pairs={{0,8},{1,9},{2,10},{3,11},{4,12},{5,13},{6,14},{7,15},{8,16},{9,17... | collective-permute-start | bytes 1572872 | tf_op jit(solution)/shard_map/ppermute | solution.py:69
  53.9 34.3 %collective-permute-start.3 = (bf16[256,1024]{1,0:T(8,128)(2,1)}, bf16[256,1024]{1,0:T(8,128)(2,1)}, u32[]{:S(2)}, u32[]{:S(2)}) collective-permute-start(bf16[256,1024]{1,0:T(8,128)(2,1)} %maximum_select_fusion.2.refs_4_.refs_9_), channel_id=1, source_target_pairs={{0,6},{1,7},{2,8},{3,9},{4,10},{5,11},{6,12},{7,13},{8,14},{9,15},... | collective-permute-start | bytes 1572872 | tf_op jit(solution)/shard_map/ppermute | solution.py:69
  60.2 38.5 %collective-permute-start.4 = (bf16[256,1024]{1,0:T(8,128)(2,1)}, bf16[256,1024]{1,0:T(8,128)(2,1)}, u32[]{:S(2)}, u32[]{:S(2)}) collective-permute-start(bf16[256,1024]{1,0:T(8,128)(2,1)} %maximum_select_fusion.2.refs_4_.refs_9_), channel_id=1, source_target_pairs={{0,4},{1,5},{2,6},{3,7},{4,8},{5,9},{6,10},{7,11},{8,12},{9,13},{1... | collective-permute-start | bytes 1572872 | tf_op jit(solution)/shard_map/ppermute | solution.py:69
  62.3 36.4 %collective-permute-start.5 = (bf16[256,1024]{1,0:T(8,128)(2,1)}, bf16[256,1024]{1,0:T(8,128)(2,1)}, u32[]{:S(2)}, u32[]{:S(2)}) collective-permute-start(bf16[256,1024]{1,0:T(8,128)(2,1)} %maximum_select_fusion.2.refs_4_.refs_9_), channel_id=1, source_target_pairs={{0,2},{1,3},{2,4},{3,5},{4,6},{5,7},{6,8},{7,9},{8,10},{9,11},{10,... | collective-permute-start | bytes 1572872 | tf_op jit(solution)/shard_map/ppermute | solution.py:69
  112.4 52.3 %collective-permute-start.10 = (bf16[256,512]{1,0:T(8,128)(2,1)S(1)}, bf16[256,512]{1,0:T(8,128)(2,1)S(1)}, u32[]{:S(2)}, u32[]{:S(2)}) collective-permute-start(bf16[256,512]{1,0:T(8,128)(2,1)S(1)} %get-tuple-element.38), channel_id=1, source_target_pairs={{0,97},{1,32},{2,99},{3,34},{4,101},{5,36},{6,103},{7,38},{8,105},... | collective-permute-start | bytes 786440 | tf_op jit(solution)/shard_map/ppermute | solution.py:36
  190.3 18.0 %collective-permute-start.19 = (bf16[128,2048]{1,0:T(8,128)(2,1)}, bf16[128,2048]{1,0:T(8,128)(2,1)S(1)}, u32[]{:S(2)}, u32[]{:S(2)}) collective-permute-start(bf16[128,2048]{1,0:T(8,128)(2,1)} %get-tuple-element.15), channel_id=1, source_target_pairs={{0,36},{1,109},{2,38},{3,111},{4,32},{5,105},{6,34},{7,107},{8,44}... | collective-permute-start | bytes 1572872 | tf_op jit(solution)/shard_map/ppermute | solution.py:36
  215.6 17.6 %collective-permute-start.28 = (bf16[2,40,4096]{2,1,0:T(8,128)(2,1)S(1)}, bf16[2,40,4096]{2,1,0:T(8,128)(2,1)S(1)}, u32[]{:S(2)}, u32[]{:S(2)}) collective-permute-start(bf16[2,40,4096]{2,1,0:T(8,128)(2,1)S(1)} %bitcast.49), channel_id=1, source_target_pairs={{0,2},{1,3},{2,0},{3,1},{4,6},{5,7},{6,4},{7,5},{8,10},{9,11},{10,... | collective-permute-start | bytes 1966088 | tf_op jit(solution)/shard_map/ppermute | solution.py:36
  215.7 30.4 %collective-permute-start.26 = (bf16[2,40,4096]{2,1,0:T(8,128)(2,1)S(1)}, bf16[2,40,4096]{2,1,0:T(8,128)(2,1)S(1)}, u32[]{:S(2)}, u32[]{:S(2)}) collective-permute-start(bf16[2,40,4096]{2,1,0:T(8,128)(2,1)S(1)} %bitcast.50), channel_id=1, source_target_pairs={{0,4},{1,5},{2,6},{3,7},{4,8},{5,9},{6,10},{7,11},{8,12},{9,13},{1... | collective-permute-start | bytes 1966088 | tf_op jit(solution)/shard_map/ppermute | solution.py:36
  217.2 29.0 %collective-permute-start.27 = (bf16[2,40,4096]{2,1,0:T(8,128)(2,1)S(1)}, bf16[2,40,4096]{2,1,0:T(8,128)(2,1)S(1)}, u32[]{:S(2)}, u32[]{:S(2)}) collective-permute-start(bf16[2,40,4096]{2,1,0:T(8,128)(2,1)S(1)} %bitcast.51), channel_id=1, source_target_pairs={{0,12},{1,13},{2,14},{3,15},{4,0},{5,1},{6,2},{7,3},{8,4},{9,5},{1... | collective-permute-start | bytes 1966088 | tf_op jit(solution)/shard_map/ppermute | solution.py:36
  219.0 29.6 %collective-permute-start.29 = (bf16[2,40,4096]{2,1,0:T(8,128)(2,1)S(1)}, bf16[2,40,4096]{2,1,0:T(8,128)(2,1)S(1)}, u32[]{:S(2)}, u32[]{:S(2)}) collective-permute-start(bf16[2,40,4096]{2,1,0:T(8,128)(2,1)S(1)} %bitcast.52), channel_id=1, source_target_pairs={{0,8},{1,9},{2,10},{3,11},{4,12},{5,13},{6,14},{7,15},{8,0},{9,1},... | collective-permute-start | bytes 1966088 | tf_op jit(solution)/shard_map/ppermute | solution.py:36
  233.3 27.9 %collective-permute-start.30 = (bf16[2,40,4096]{2,1,0:T(8,128)(2,1)S(1)}, bf16[2,40,4096]{2,1,0:T(8,128)(2,1)S(1)}, u32[]{:S(2)}, u32[]{:S(2)}) collective-permute-start(bf16[2,40,4096]{2,1,0:T(8,128)(2,1)S(1)} %collective-permute-done.28), channel_id=1, source_target_pairs={{0,4},{1,5},{2,6},{3,7},{4,8},{5,9},{6,10},{7,11},{8,12},{9,13},{1... | collective-permute-start | bytes 1966088 | tf_op jit(solution)/shard_map/ppermute | solution.py:36
  246.5 20.7 %collective-permute-start.33 = (bf16[2,160,4096]{2,1,0:T(8,128)(2,1)S(1)}, bf16[2,160,4096]{2,1,0:T(8,128)(2,1)S(1)}, u32[]{:S(2)}, u32[]{:S(2)}) collective-permute-start(bf16[2,160,4096]{2,1,0:T(8,128)(2,1)S(1)} %pad_maximum_fusion.refs_0_), channel_id=1, source_target_pairs={{0,1},{1,0},{2,3},{3,2},{4,5},{5,4},{6,7},{7,6},{8,9},{9,8},{10,11... | collective-permute-start | bytes 7864328 | tf_op jit(solution)/shard_map/ppermute | solution.py:36
  246.6 17.1 %collective-permute-start.31 = (bf16[2,40,4096]{2,1,0:T(8,128)(2,1)S(1)}, bf16[2,40,4096]{2,1,0:T(8,128)(2,1)S(1)}, u32[]{:S(2)}, u32[]{:S(2)}) collective-permute-start(bf16[2,40,4096]{2,1,0:T(8,128)(2,1)S(1)} %collective-permute-done.28), channel_id=1, source_target_pairs={{0,12},{1,13},{2,14},{3,15},{4,0},{5,1},{6,2},{7,3},{8,4},{9,5},{1... | collective-permute-start | bytes 1966088 | tf_op jit(solution)/shard_map/ppermute | solution.py:36
  248.6 18.3 %collective-permute-start.32 = (bf16[2,40,4096]{2,1,0:T(8,128)(2,1)S(1)}, bf16[2,40,4096]{2,1,0:T(8,128)(2,1)S(1)}, u32[]{:S(2)}, u32[]{:S(2)}) collective-permute-start(bf16[2,40,4096]{2,1,0:T(8,128)(2,1)S(1)} %collective-permute-done.29), channel_id=1, source_target_pairs={{0,2},{1,3},{2,0},{3,1},{4,6},{5,7},{6,4},{7,5},{8,10},{9,11},{10,... | collective-permute-start | bytes 1966088 | tf_op jit(solution)/shard_map/ppermute | solution.py:36
  314.2 17.7 %collective-permute-start.38 = (bf16[2,40,4096]{2,1,0:T(8,128)(2,1)S(1)}, bf16[2,40,4096]{2,1,0:T(8,128)(2,1)S(1)}, u32[]{:S(2)}, u32[]{:S(2)}) collective-permute-start(bf16[2,40,4096]{2,1,0:T(8,128)(2,1)S(1)} %get-tuple-element.32), channel_id=1, source_target_pairs={{0,12},{1,13},{2,14},{3,15},{4,0},{5,1},{6,2},{7,3},{8,4},{9,5},{1... | collective-permute-start | bytes 1966088 | tf_op jit(solution)/shard_map/ppermute | solution.py:36
  314.3 18.9 %collective-permute-start.39 = (bf16[2,40,4096]{2,1,0:T(8,128)(2,1)S(1)}, bf16[2,40,4096]{2,1,0:T(8,128)(2,1)S(1)}, u32[]{:S(2)}, u32[]{:S(2)}) collective-permute-start(bf16[2,40,4096]{2,1,0:T(8,128)(2,1)S(1)} %get-tuple-element.31), channel_id=1, source_target_pairs={{0,4},{1,5},{2,6},{3,7},{4,8},{5,9},{6,10},{7,11},{8,12},{9,13},{1... | collective-permute-start | bytes 1966088 | tf_op jit(solution)/shard_map/ppermute | solution.py:36
  316.3 17.8 %collective-permute-start.41 = (bf16[2,40,4096]{2,1,0:T(8,128)(2,1)S(1)}, bf16[2,40,4096]{2,1,0:T(8,128)(2,1)S(1)}, u32[]{:S(2)}, u32[]{:S(2)}) collective-permute-start(bf16[2,40,4096]{2,1,0:T(8,128)(2,1)S(1)} %get-tuple-element.30), channel_id=1, source_target_pairs={{0,2},{1,3},{2,0},{3,1},{4,6},{5,7},{6,4},{7,5},{8,10},{9,11},{10,... | collective-permute-start | bytes 1966088 | tf_op jit(solution)/shard_map/ppermute | solution.py:36
  319.5 26.4 %collective-permute-start.36 = (bf16[2,40,4096]{2,1,0:T(8,128)(2,1)S(1)}, bf16[2,40,4096]{2,1,0:T(8,128)(2,1)S(1)}, u32[]{:S(2)}, u32[]{:S(2)}) collective-permute-start(bf16[2,40,4096]{2,1,0:T(8,128)(2,1)S(1)} %get-tuple-element.29), channel_id=1, source_target_pairs={{0,12},{1,13},{2,14},{3,15},{4,0},{5,1},{6,2},{7,3},{8,4},{9,5},{1... | collective-permute-start | bytes 1966088 | tf_op jit(solution)/shard_map/ppermute | solution.py:36
  320.8 25.9 %collective-permute-start.37 = (bf16[2,40,4096]{2,1,0:T(8,128)(2,1)S(1)}, bf16[2,40,4096]{2,1,0:T(8,128)(2,1)S(1)}, u32[]{:S(2)}, u32[]{:S(2)}) collective-permute-start(bf16[2,40,4096]{2,1,0:T(8,128)(2,1)S(1)} %get-tuple-element.33), channel_id=1, source_target_pairs={{0,4},{1,5},{2,6},{3,7},{4,8},{5,9},{6,10},{7,11},{8,12},{9,13},{1... | collective-permute-start | bytes 1966088 | tf_op jit(solution)/shard_map/ppermute | solution.py:36
  339.4 21.5 %collective-permute-start.42 = (bf16[2,40,4096]{2,1,0:T(8,128)(2,1)S(1)}, bf16[2,40,4096]{2,1,0:T(8,128)(2,1)S(1)}, u32[]{:S(2)}, u32[]{:S(2)}) collective-permute-start(bf16[2,40,4096]{2,1,0:T(8,128)(2,1)S(1)} %get-tuple-element.35), channel_id=1, source_target_pairs={{0,8},{1,9},{2,10},{3,11},{4,12},{5,13},{6,14},{7,15},{8,0},{9,1},... | collective-permute-start | bytes 1966088 | tf_op jit(solution)/shard_map/ppermute | solution.py:36
  (40 other events, 484.5 us)
